TPU v7x, 8 devices: a whole 2x2x1 slice. The times are simulated.
8 devices in a mesh: stage: 2 (over z, y), data: 4 (over x, core).
Axes of the slice: x: 2, y: 2, z: 1, core: 2. Of those that a mesh axis runs over, the one named last changes fastest.
Arguments:
- x_in: bfloat16 [32, 2048, 768], P(None, 'data')
- targets: bfloat16 [32, 2048, 768], P(None, 'data')
- w1_bf: bfloat16 [2, 2, 1, 768, 3072], P('stage')
- w2_bf: bfloat16 [2, 2, 1, 3072, 768], P('stage')
- w_master: float32 [2, 2, 1, 4718592], P('stage', None, None, 'data')
- m_state: float32 [2, 2, 1, 4718592], P('stage', None, None, 'data')
- v_state: float32 [2, 2, 1, 4718592], P('stage', None, None, 'data')
Outputs:
- output 1: bfloat16 [2, 2, 1, 768, 3072], P('stage')
- output 2: bfloat16 [2, 2, 1, 3072, 768], P('stage')
- output 3: float32 [2, 2, 1, 4718592], P('stage', None, None, 'data')
- output 4: float32 [2, 2, 1, 4718592], P('stage', None, None, 'data')
- output 5: float32 [2, 2, 1, 4718592], P('stage', None, None, 'data')
- output 6: float32 [], replicated
All inputs are finite; a program needn't handle non-finite values.
Results may differ from a plain program's by a relative error of at most 0.001.
Values are sent between devices in bfloat16 or wider.
A program may use at most 1 GiB of HBM per device.

v0:
```python
import math
import jax
import jax.numpy as jnp
from jax import lax
from jax.sharding import PartitionSpec as P

BETA_ONE = 0.9
BETA_TWO = 0.999
ADAM_EPS = 1e-8
WEIGHT_DECAY = 0.1
ADAM_STEP = 1000


def gelu_tanh(pre_act):
    return jax.nn.gelu(pre_act, approximate=True)


def block_forward(h_in, w_one, w_two):
    pre_act = jnp.dot(h_in, w_one, preferred_element_type=jnp.float32)
    act_bf = gelu_tanh(pre_act).astype(jnp.bfloat16)
    out_val = h_in.astype(jnp.float32) + jnp.dot(act_bf, w_two, preferred_element_type=jnp.float32)
    return out_val.astype(jnp.bfloat16)


def block_backward(h_in, grad_out, w_one, w_two):
    pre_act = jnp.dot(h_in, w_one, preferred_element_type=jnp.float32)
    act_val, gelu_pull = jax.vjp(gelu_tanh, pre_act)
    grad_act = jnp.einsum("td,fd->tf", grad_out, w_two, preferred_element_type=jnp.float32)
    grad_pre = gelu_pull(grad_act)[0].astype(jnp.bfloat16)
    back_val = jnp.einsum("tf,df->td", grad_pre, w_one, preferred_element_type=jnp.float32)
    grad_in = (grad_out.astype(jnp.float32) + back_val).astype(jnp.bfloat16)
    grad_one = jnp.einsum("td,tf->df", h_in, grad_pre, preferred_element_type=jnp.float32)
    grad_two = jnp.einsum("tf,td->fd", act_val.astype(jnp.bfloat16), grad_out, preferred_element_type=jnp.float32)
    return grad_in, grad_one, grad_two


def adam_update(w_old, m_old, v_old, grad_val, clip_factor, learn_rate):
    grad_clip = clip_factor * grad_val
    m_new = BETA_ONE * m_old + (1.0 - BETA_ONE) * grad_clip
    v_new = BETA_TWO * v_old + (1.0 - BETA_TWO) * grad_clip * grad_clip
    m_hat = m_new / (1.0 - BETA_ONE ** ADAM_STEP)
    v_hat = v_new / (1.0 - BETA_TWO ** ADAM_STEP)
    w_new = w_old - learn_rate * (m_hat / (jnp.sqrt(v_hat) + ADAM_EPS) + WEIGHT_DECAY * w_old)
    return w_new, m_new, v_new


def item_coords(item_idx, n_stage, backward):
    group_idx = item_idx // (2 * n_stage)
    within = item_idx % (2 * n_stage)
    half_idx = within // n_stage
    if backward:
        half_idx = 1 - half_idx
    return half_idx, group_idx * n_stage + within % n_stage


def run_stack(x_loc, t_loc, w_ones, w_twos, n_stage, n_tokens):
    stage_idx = lax.axis_index("stage")
    n_micro, n_tok, d_model = x_loc.shape
    n_blk, d_ff = w_ones.shape[1], w_ones.shape[3]
    n_items = 2 * n_micro
    n_ticks = n_items + n_stage - 1
    fwd_perm = [(src, (src + 1) % n_stage) for src in range(n_stage)]
    bwd_perm = [(src, (src - 1) % n_stage) for src in range(n_stage)]

    def fwd_tick(tick_idx, state_carry):
        recv_act, saved_in, seed_buf, loss_acc = state_carry
        item_idx = tick_idx - stage_idx
        active = (item_idx >= 0) & (item_idx < n_items)
        half_idx, micro_idx = item_coords(jnp.clip(item_idx, 0, n_items - 1), n_stage, False)
        slot_idx = jnp.where(active, micro_idx, n_micro)
        x_mb = lax.dynamic_index_in_dim(x_loc, micro_idx, 0, keepdims=False)
        h_cur = jnp.where((half_idx == 0) & (stage_idx == 0), x_mb, recv_act)
        half_one = lax.dynamic_index_in_dim(w_ones, half_idx, 0, keepdims=False)
        half_two = lax.dynamic_index_in_dim(w_twos, half_idx, 0, keepdims=False)
        for block_idx in range(n_blk):
            saved_in = lax.dynamic_update_slice(saved_in, h_cur[None, None, None], (half_idx, slot_idx, block_idx, 0, 0))
            h_cur = block_forward(h_cur, half_one[block_idx], half_two[block_idx])
        is_last = active & (half_idx == 1) & (stage_idx == n_stage - 1)
        t_mb = lax.dynamic_index_in_dim(t_loc, micro_idx, 0, keepdims=False)
        residual = h_cur.astype(jnp.float32) - t_mb.astype(jnp.float32)
        loss_acc = loss_acc + jnp.where(is_last, 0.5 * jnp.sum(residual * residual), 0.0)
        seed_slot = jnp.where(is_last, micro_idx, n_micro)
        seed_buf = lax.dynamic_update_slice(seed_buf, (residual / n_tokens).astype(jnp.bfloat16)[None], (seed_slot, 0, 0))
        recv_act = lax.ppermute(h_cur, "stage", fwd_perm)
        return recv_act, saved_in, seed_buf, loss_acc

    fwd_start = (jnp.zeros((n_tok, d_model), jnp.bfloat16), jnp.zeros((2, n_micro + 1, n_blk, n_tok, d_model), jnp.bfloat16), jnp.zeros((n_micro + 1, n_tok, d_model), jnp.bfloat16), jnp.zeros((), jnp.float32))
    fwd_out = lax.fori_loop(0, n_ticks, fwd_tick, fwd_start)
    saved_in, seed_buf, loss_acc = fwd_out[1], fwd_out[2], fwd_out[3]

    def bwd_tick(tick_idx, state_carry):
        recv_grad, acc_one, acc_two = state_carry
        item_idx = tick_idx - (n_stage - 1 - stage_idx)
        active = (item_idx >= 0) & (item_idx < n_items)
        half_idx, micro_idx = item_coords(jnp.clip(item_idx, 0, n_items - 1), n_stage, True)
        seed_mb = lax.dynamic_index_in_dim(seed_buf, micro_idx, 0, keepdims=False)
        is_seed = (half_idx == 1) & (stage_idx == n_stage - 1)
        grad_cur = jnp.where(is_seed, seed_mb, recv_grad)
        grad_cur = jnp.where(active, grad_cur, jnp.zeros_like(grad_cur))
        half_one = lax.dynamic_index_in_dim(w_ones, half_idx, 0, keepdims=False)
        half_two = lax.dynamic_index_in_dim(w_twos, half_idx, 0, keepdims=False)
        saved_mb = lax.dynamic_slice(saved_in, (half_idx, micro_idx, 0, 0, 0), (1, 1, n_blk, n_tok, d_model))[0, 0]
        for block_idx in reversed(range(n_blk)):
            grad_cur, grad_one, grad_two = block_backward(saved_mb[block_idx], grad_cur, half_one[block_idx], half_two[block_idx])
            old_one = lax.dynamic_slice(acc_one, (half_idx, block_idx, 0, 0), (1, 1, d_model, d_ff))
            acc_one = lax.dynamic_update_slice(acc_one, old_one + grad_one[None, None], (half_idx, block_idx, 0, 0))
            old_two = lax.dynamic_slice(acc_two, (half_idx, block_idx, 0, 0), (1, 1, d_ff, d_model))
            acc_two = lax.dynamic_update_slice(acc_two, old_two + grad_two[None, None], (half_idx, block_idx, 0, 0))
        recv_grad = lax.ppermute(grad_cur, "stage", bwd_perm)
        return recv_grad, acc_one, acc_two

    bwd_start = (jnp.zeros((n_tok, d_model), jnp.bfloat16), jnp.zeros((2, n_blk, d_model, d_ff), jnp.float32), jnp.zeros((2, n_blk, d_ff, d_model), jnp.float32))
    bwd_out = lax.fori_loop(0, n_ticks, bwd_tick, bwd_start)
    return bwd_out[1], bwd_out[2], loss_acc


def solution(mesh):
    n_stage = mesh.shape["stage"]
    n_data = mesh.shape["data"]

    def device_step(x_loc, t_loc, w1_loc, w2_loc, wm_loc, m_loc, v_loc):
        n_micro, n_tok, d_model = x_loc.shape
        n_blk, d_ff = w1_loc.shape[2], w1_loc.shape[4]
        n_tokens = n_micro * n_tok * n_data
        n_blocks = 2 * n_stage * n_blk
        tau_clip = 0.3 * d_model * math.sqrt(n_blocks * (3.0 / n_tokens + 0.008))
        learn_rate = 0.1 / math.sqrt(4.0 * d_model * n_blocks)
        acc_one, acc_two, loss_acc = run_stack(x_loc, t_loc, w1_loc[0], w2_loc[0], n_stage, n_tokens)
        grad_flat = jnp.concatenate([acc_one.reshape(2, n_blk, -1), acc_two.reshape(2, n_blk, -1)], axis=-1)
        grad_shard = lax.psum_scatter(grad_flat, "data", scatter_dimension=2, tiled=True)
        grad_norm = jnp.sqrt(lax.psum(jnp.sum(grad_shard * grad_shard), ("stage", "data")))
        clip_factor = jnp.minimum(1.0, tau_clip / grad_norm)
        w_new, m_new, v_new = adam_update(wm_loc[0], m_loc[0], v_loc[0], grad_shard, clip_factor, learn_rate)
        w_full = lax.all_gather(w_new.astype(jnp.bfloat16), "data", axis=2, tiled=True)
        split_at = d_model * d_ff
        w1_new = w_full[:, :, :split_at].reshape(1, 2, n_blk, d_model, d_ff)
        w2_new = w_full[:, :, split_at:].reshape(1, 2, n_blk, d_ff, d_model)
        mean_loss = lax.psum(loss_acc, ("stage", "data")) / n_tokens
        return w1_new, w2_new, w_new[None], m_new[None], v_new[None], mean_loss

    act_spec = P(None, "data", None)
    flat_spec = P("stage", None, None, "data")
    return jax.shard_map(device_step, mesh=mesh, in_specs=(act_spec, act_spec, P("stage"), P("stage"), flat_spec, flat_spec, flat_spec), out_specs=(P("stage"), P("stage"), flat_spec, flat_spec, flat_spec, P()), check_vma=False)
```

profile of v0, /device:TPU:0, one launch (start us, length us, event | category | flops | bytes accessed | tf_op | source)
XLA Modules:
  0.0 5532.2 jit_solution(241884022216018079)
XLA Ops:
  7.2 16.6 broadcast_in_dim.67
  32.7 1681.1 %while.42 = (s32[]{:T(128)}, bf16[512,768]{1,0:T(8,128)(2,1)S(1)}, bf16[2,33,1,512,768]{4,3,2,1,0:T(8,128)(2,1)}, bf16[33,512,768]{2,1,0:T(8,128)(2,1)}, f32[]{:...) while((s32[]{:T(128)}, bf16[512,768]{1,0:T(8,128)(2,1)S(1)}, ...), condition=%wide.region_2.3_spmd, body=%wide.region_0.2_spmd.sunk | while | flops 4852285440 | bytes 23597420 | solution.py:88
  507.4 12.6 collective-permute-done
  535.9 13.7 collective-permute-done
  565.5 14.8 collective-permute-done
  596.2 14.5 collective-permute-done
  626.8 13.4 collective-permute-done
  1141.3 13.4 collective-permute-done
  1172.3 12.7 collective-permute-done
  1731.2 2498.4 %while.43 = (s32[]{:T(128)}, bf16[512,768]{1,0:T(8,128)(2,1)}, f32[2,1,768,3072]{3,2,1,0:T(8,128)}, f32[2,1,3072,768]{3,2,1,0:T(8,128)}, s32[]{:T(128)}, /*index...) while((s32[]{:T(128)}, bf16[512,768]{1,0:T(8,128)(2,1)}, ...), condition=%wide.region_4.5_spmd, body=%wide.region_3.4_spmd.sunk | while | flops 12131893248 | bytes 181669712 | solution.py:113
  1750.3 12.6 fusion.117
  1788.0 12.6 fusion.117
  1827.6 12.6 fusion.117
  1904.0 12.5 fusion.117
  1941.7 12.6 fusion.117
  1981.3 12.6 fusion.117
  2018.9 12.5 fusion.117
  2057.7 12.5 fusion.117
  2095.3 12.6 fusion.117
  2134.9 12.6 fusion.117
  2172.6 12.5 fusion.117
  2249.1 12.6 fusion.117
  2288.5 12.6 fusion.117
  2326.3 12.5 fusion.117
  2402.7 12.6 fusion.117
  2442.2 12.6 fusion.117
  2556.4 12.6 fusion.117
  2595.8 12.6 fusion.117
  2672.3 12.5 fusion.117
  2710.0 12.6 fusion.117
  2749.6 12.6 fusion.117
  2787.3 12.5 fusion.117
  2826.0 12.5 fusion.117
  2863.7 12.6 fusion.117
  2903.2 12.6 fusion.117
  2979.6 12.5 fusion.117
  3017.3 12.6 fusion.117
  3056.8 12.6 fusion.117
  3171.0 12.6 fusion.117
  3210.5 12.6 fusion.117
  3248.2 12.5 fusion.117
  3324.6 12.6 fusion.117
  3364.1 12.6 fusion.117
  3401.8 12.5 fusion.117
  3440.5 12.5 fusion.117
  3478.3 12.6 fusion.117
  3517.7 12.6 fusion.117
  3631.9 12.6 fusion.117
  3671.4 12.6 fusion.117
  3785.5 12.6 fusion.117
  3825.0 12.6 fusion.117
  3939.2 12.6 fusion.117
  3978.6 12.6 fusion.117
  4092.8 12.6 fusion.117
  4132.3 12.6 fusion.117
  4229.6 40.6 reshape.70
  4270.3 37.2 reshape.71
  4307.5 101.8 %pad_maximum_fusion = f32[2,1,4718592]{2,1,0:T(1,128)} fusion(f32[2,1,2359296]{2,1,0:T(1,128)} %reshape.71, f32[2,1,2359296]{2,1,0:T(1,128)} %reshape.70), kind=kLoop, calls=%fused_computation.73 | loop fusion | flops 9437184 | bytes 75497472 | tf_op jit(solution)/shard_map/concatenate | solution.py:129
  4411.2 622.2 %all-reduce.4.cloned.1.call-done = f32[2,1,4718592]{2,1,0:T(1,128)} async-done(((f32[2,1,4718592]{2,1,0:T(1,128)}), f32[2,1,4718592]{2,1,0:T(1,128)}) %all-reduce.4.cloned.1.call-update) | async-done | bytes 37748752
  5033.4 21.2 multiply_reduce_fusion.1
  5054.6 23.3 all-reduce.1
  5078.6 73.6 %fusion.78 = (bf16[2,1,1179648]{2,1,0:T(2,128)(2,1)}, f32[2,1,1179648]{2,1,0:T(1,128)}, f32[2,1,1179648]{2,1,0:T(1,128)}, f32[2,1,1179648]{2,1,0:T(1,128)}) fusion(f32[1,2,1,1179648]{3,2,1,0:T(1,128)} %param.15, f32[2,1,4718592]{2,1,0:T(1,128)} %all-reduce.4.cloned.1.call-done, u32[]{:T(128)S(6)} %multiply.25, f32[]{:T(128)S(6)} %min.26, ...), kind=kLoop, calls=%fused_computation.86 | loop fusion | flops 37748736 | bytes 70778888 | tf_op jit(solution)/shard_map/convert_element_type | solution.py:134
  5152.9 228.5 %all-gather.2.cloned.1.call-done = bf16[2,1,4718592]{2,1,0:T(2,128)(2,1)} async-done(((bf16[2,1,1179648]{2,1,0:T(2,128)(2,1)}), bf16[2,1,4718592]{2,1,0:T(2,128)(2,1)}) %all-gather.2.cloned.1.call-update) | async-done | bytes 18874384 | tf_op jit(solution)/shard_map/all_gather | solution.py:134
  5381.4 123.5 %slice_reduce_fusion = (bf16[2,2359296]{1,0:T(2,128)(2,1)}, bf16[2,2359296]{1,0:T(2,128)(2,1)}) fusion(bf16[2,1,4718592]{2,1,0:T(2,128)(2,1)} %all-gather.2.cloned.1.call-done), kind=kLoop, calls=%fused_computation.74 | loop fusion | bytes 37748736 | tf_op jit(solution)/shard_map/slice | solution.py:137
  (1587 shorter events, 3508.9 us)
Async XLA Ops:
  7.2 5026.3 %all-reduce.4.cloned.1.call-start = ((), (), s32[]{:S(2)}) async-start(), calls=%async_computation.1 | async-start | bytes 75497472
  43.4 20.9 collective-permute-start
  1134.3 20.4 collective-permute-start
  1749.2 21.4 collective-permute-start.1
  1788.0 20.2 collective-permute-start.1
  1825.6 22.2 collective-permute-start.1
  1902.9 21.3 collective-permute-start.1
  1941.6 20.3 collective-permute-start.1
  1979.3 22.2 collective-permute-start.1
  2056.5 21.3 collective-permute-start.1
  2095.2 20.3 collective-permute-start.1
  2133.0 22.1 collective-permute-start.1
  2172.5 20.3 collective-permute-start.1
  2210.3 21.2 collective-permute-start.1
  2248.9 20.4 collective-permute-start.1
  2286.7 22.0 collective-permute-start.1
  2326.2 20.3 collective-permute-start.1
  2363.9 21.2 collective-permute-start.1
  2402.5 20.4 collective-permute-start.1
  2440.4 22.0 collective-permute-start.1
  2479.8 20.3 collective-permute-start.1
  2517.5 21.2 collective-permute-start.1
  2556.1 20.4 collective-permute-start.1
  2594.0 22.0 collective-permute-start.1
  2633.4 20.3 collective-permute-start.1
  2671.2 21.3 collective-permute-start.1
  2709.9 20.3 collective-permute-start.1
  2747.7 22.1 collective-permute-start.1
  2824.8 21.3 collective-permute-start.1
  2863.5 20.4 collective-permute-start.1
  2901.3 22.1 collective-permute-start.1
  2978.5 21.3 collective-permute-start.1
  3017.2 20.4 collective-permute-start.1
  3055.0 22.1 collective-permute-start.1
  3132.1 21.2 collective-permute-start.1
  3170.8 20.4 collective-permute-start.1
  3208.6 22.1 collective-permute-start.1
  3248.1 20.2 collective-permute-start.1
  3285.8 21.2 collective-permute-start.1
  3324.4 20.4 collective-permute-start.1
  3362.2 22.1 collective-permute-start.1
  3401.7 20.2 collective-permute-start.1
  3439.4 21.2 collective-permute-start.1
  3478.1 20.4 collective-permute-start.1
  3515.9 22.1 collective-permute-start.1
  3555.4 20.3 collective-permute-start.1
  3593.1 21.2 collective-permute-start.1
  3631.7 20.4 collective-permute-start.1
  3669.5 22.0 collective-permute-start.1
  3709.0 20.3 collective-permute-start.1
  3746.7 21.2 collective-permute-start.1
  3785.3 20.4 collective-permute-start.1
  3823.2 22.0 collective-permute-start.1
  3862.6 20.3 collective-permute-start.1
  3900.3 21.2 collective-permute-start.1
  3939.0 20.4 collective-permute-start.1
  3976.8 22.0 collective-permute-start.1
  4016.3 20.3 collective-permute-start.1
  4054.0 21.2 collective-permute-start.1
  4092.6 20.4 collective-permute-start.1
  4130.5 22.0 collective-permute-start.1
  4169.9 20.3 collective-permute-start.1
  4207.6 22.0 collective-permute-start.1
  4409.4 972.1 %all-gather.2.cloned.1.call-start = ((), (), s32[]{:S(2)}) async-start(), calls=%async_computation | async-start | bytes 47185920 | tf_op jit(solution)/shard_map/all_gather | solution.py:134
  (394 other events, 3525.1 us)
Sparse Core Ops, SparseCore 0:
  4409.5 623.9 all-reduce.3
  5152.4 229.0 all-gather.1
where the time goes:
time: 5550 us; the launch traced here: 5530 us
  matrix products  2940 us (53%)
  waiting for transfers between devices  1430 us (26%)
  other arithmetic  666 us (12%)
  local copies, waits for them, and re-layouts  270 us (5%)
  starting transfers between devices  122 us (2%)
  loops' own time  57.7 us (1%)
    dot_general x65, matrix products, block_backward(): jnp.einsum('tf,td->fd', act_val.astype(jnp.bfloat16), grad_out, preferred...  813 us
    dot_general x65, matrix products, block_forward(): jnp.dot(act_bf, w_two, preferred_element_type=jnp.float32)  687 us
    unnamed x3, waiting for transfers between devices  622 us
    ppermute x65, waiting for transfers between devices, fwd_tick(): recv_act = lax.ppermute(h_cur, 'stage', fwd_perm)  584 us
    dot_general x65, matrix products, block_backward(): jnp.einsum('td,tf->df', h_in, grad_pre, preferred_element_type=jnp.float32)  498 us
    dot_general x65, matrix products, block_backward(): jnp.einsum('td,fd->tf', grad_out, w_two, preferred_element_type=jnp.float32)  401 us
    dot_general x65, matrix products, block_backward(): pre_act = jnp.dot(h_in, w_one, preferred_element_type=jnp.float32)  313 us
    dot_general x65, matrix products, block_backward(): jnp.einsum('tf,df->td', grad_pre, w_one, preferred_element_type=jnp.float32)  229 us
  transfers between devices with their start and end apart: 132, of which 68 were waited for; matrix products, arithmetic and copies ran while one was open for 29% of the time, Pallas kernels for 0%

commit v1 on v0

v1 whole, which is shorter than its diff:
```python
import math
import jax
import jax.numpy as jnp
from jax import lax
from jax.experimental import pallas as pl
from jax.experimental.pallas import tpu as pltpu
from jax.sharding import PartitionSpec as P

BETA_ONE = 0.9
BETA_TWO = 0.999
ADAM_EPS = 1e-8
WEIGHT_DECAY = 0.1
ADAM_STEP = 1000
BF = jnp.bfloat16
F32 = jnp.float32
K_GELU = math.sqrt(2.0 / math.pi)
C_GELU = 0.044715
ANY = pl.ANY
TM = 512
N_PART = 3
VMEM_CAP = 60 * 1024 * 1024


def dot_nn(lhs, rhs):
    return lax.dot_general(lhs, rhs, (((1,), (0,)), ((), ())), preferred_element_type=F32)


def dot_nt(lhs, rhs):
    return lax.dot_general(lhs, rhs, (((1,), (1,)), ((), ())), preferred_element_type=F32)


def dot_tn(lhs, rhs):
    return lax.dot_general(lhs, rhs, (((0,), (0,)), ((), ())), preferred_element_type=F32)


def gelu_and_slope(u):
    sq = u * u
    half = 0.5 + 0.5 * jnp.tanh(u * (K_GELU + (K_GELU * C_GELU) * sq))
    act = u * half
    slope = half + (act * (1.0 - half)) * (2.0 * K_GELU + (6.0 * K_GELU * C_GELU) * sq)
    return act, slope


def row_spec(width, moved=False):
    if moved:
        return pl.BlockSpec((TM, width), lambda i, off: (i + off[0], 0))
    return pl.BlockSpec((TM, width), lambda i, off: (i, 0))


def weight_spec(r, c, which):
    return pl.BlockSpec((None, r, c), lambda i, off: (which, 0, 0), pipeline_mode=pl.Buffered(1))


def fwd_call(first, x, w_one, w_two, which, n_row, targets=None, n_tokens=None, chunk=1024):
    d_model = x.shape[1]
    d_ff = w_one.shape[2]
    last = targets is not None

    def kernel(off_ref, x_ref, w1_ref, w2_ref, *rest):
        if last:
            t_ref, h_ref, a_ref, s_ref, loss_ref = rest
        else:
            h_ref, a_ref, s_ref = rest
        acc = x_ref[...].astype(F32)
        pre = dot_nn(x_ref[...], w1_ref[:, :chunk])
        for lo in range(0, d_ff, chunk):
            cols = slice(lo, lo + chunk)
            ahead = dot_nn(x_ref[...], w1_ref[:, lo + chunk:lo + 2 * chunk]) if lo + chunk < d_ff else None
            act, slope = gelu_and_slope(pre)
            act = act.astype(BF)
            a_ref[:, cols] = act
            s_ref[:, cols] = slope
            acc = acc + dot_nn(act, w2_ref[cols, :])
            pre = ahead
        out = acc.astype(BF)
        if not last:
            h_ref[...] = out
        else:
            residual = out.astype(F32) - t_ref[...].astype(F32)
            h_ref[...] = (residual / n_tokens).astype(BF)
            part = jnp.sum((residual * residual).reshape(TM // 8, 8, d_model), axis=0)

            @pl.when(pl.program_id(0) == 0)
            def _():
                loss_ref[...] = part

            @pl.when(pl.program_id(0) > 0)
            def _():
                loss_ref[...] += part

    out_specs = [row_spec(d_model), row_spec(d_ff), row_spec(d_ff)]
    out_shape = [jax.ShapeDtypeStruct((n_row, d_model), BF), jax.ShapeDtypeStruct((n_row, d_ff), BF), jax.ShapeDtypeStruct((n_row, d_ff), F32)]
    if last:
        out_specs.append(pl.BlockSpec((8, d_model), lambda i, off: (0, 0)))
        out_shape.append(jax.ShapeDtypeStruct((8, d_model), F32))
    return pl.pallas_call(
        kernel,
        grid_spec=pltpu.PrefetchScalarGridSpec(
            num_scalar_prefetch=1, grid=(n_row // TM,),
            in_specs=[row_spec(d_model), weight_spec(d_model, d_ff, which), weight_spec(d_ff, d_model, which)] + ([row_spec(d_model, True)] if last else []),
            out_specs=out_specs),
        out_shape=out_shape,
        compiler_params=pltpu.CompilerParams(vmem_limit_bytes=VMEM_CAP, dimension_semantics=("arbitrary",)),
        cost_estimate=pl.CostEstimate(flops=4 * n_row * d_model * d_ff, bytes_accessed=n_row * d_ff * 6, transcendentals=n_row * d_ff),
        name="block_fwd",
    )(first, x, w_one, w_two, *([targets] if last else []))


def up_call(first, x, w_one, which, n_row, chunk=1024):
    d_model = x.shape[1]
    d_ff = w_one.shape[2]

    def kernel(off_ref, x_ref, w1_ref, a_ref, s_ref):
        for lo in range(0, d_ff, chunk):
            cols = slice(lo, lo + chunk)
            act, slope = gelu_and_slope(dot_nn(x_ref[...], w1_ref[:, cols]))
            a_ref[:, cols] = act.astype(BF)
            s_ref[:, cols] = slope

    return pl.pallas_call(
        kernel,
        grid_spec=pltpu.PrefetchScalarGridSpec(
            num_scalar_prefetch=1, grid=(n_row // TM,),
            in_specs=[row_spec(d_model, True), weight_spec(d_model, d_ff, which)],
            out_specs=[row_spec(d_ff), row_spec(d_ff)]),
        out_shape=[jax.ShapeDtypeStruct((n_row, d_ff), BF), jax.ShapeDtypeStruct((n_row, d_ff), F32)],
        compiler_params=pltpu.CompilerParams(vmem_limit_bytes=VMEM_CAP, dimension_semantics=("arbitrary",)),
        cost_estimate=pl.CostEstimate(flops=2 * n_row * d_model * d_ff, bytes_accessed=n_row * d_ff * 6, transcendentals=n_row * d_ff),
        name="block_up",
    )(first, x, w_one)


def down_call(first, x, act, w_two, which, n_row):
    d_model = x.shape[1]
    d_ff = w_two.shape[1]

    def kernel(off_ref, x_ref, a_ref, w2_ref, h_ref):
        h_ref[...] = (x_ref[...].astype(F32) + dot_nn(a_ref[...], w2_ref[...])).astype(BF)

    return pl.pallas_call(
        kernel,
        grid_spec=pltpu.PrefetchScalarGridSpec(
            num_scalar_prefetch=1, grid=(n_row // TM,),
            in_specs=[row_spec(d_model, True), row_spec(d_ff), weight_spec(d_ff, d_model, which)],
            out_specs=row_spec(d_model)),
        out_shape=jax.ShapeDtypeStruct((n_row, d_model), BF),
        compiler_params=pltpu.CompilerParams(vmem_limit_bytes=VMEM_CAP, dimension_semantics=("arbitrary",)),
        cost_estimate=pl.CostEstimate(flops=2 * n_row * d_model * d_ff, bytes_accessed=n_row * d_ff * 2, transcendentals=0),
        name="block_down",
    )(first, x, act, w_two)


def bwd_call(first, x, grad, act, slope, w_one, w_two, which, pair, n_part=1, chunk=1024):
    n_row, d_model = grad.shape
    d_ff = w_one.shape[2]
    n_step = n_row // TM
    lanes = d_ff // 128
    major = d_model // 8
    per = d_ff // d_model
    part_lanes = lanes // n_part
    pair_shape = (2, 2, major, part_lanes, 8, 128)

    def kernel(off_ref, x_ref, g_ref, a_ref, s_ref, w1_ref, w2_ref, *rest):
        if pair is not None:
            rest = rest[n_part:]
        gin_ref, pair_refs, (acc1, acc2, sem) = rest[0], rest[1:1 + n_part], rest[1 + n_part:]
        step = pl.program_id(0)

        @pl.when(step == 0)
        def _():
            acc1[...] = jnp.zeros_like(acc1)
            acc2[...] = jnp.zeros_like(acc2)

        back = g_ref[...].astype(F32)
        for lo in range(0, d_ff, chunk):
            cols = slice(lo, lo + chunk)
            r = (dot_nt(g_ref[...], w2_ref[cols, :]) * s_ref[:, cols]).astype(BF)
            acc1[:, :, cols] += dot_tn(x_ref[...], r).reshape(major, 8, chunk)
            n_grp = chunk // (8 * per)
            acc2[lo // (8 * per):lo // (8 * per) + n_grp] += dot_tn(a_ref[:, cols], g_ref[...]).reshape(n_grp, per, 8, d_model)
            back = back + dot_nt(r, w1_ref[:, cols])
        gin_ref[...] = back.astype(BF)

        @pl.when(step == n_step - 1)
        def _():
            copies = []
            for lane in range(lanes):
                part, slot = lane // part_lanes, lane % part_lanes
                wide = part_lanes // per
                col = part * wide + slot % wide
                copies.append(pltpu.make_async_copy(acc1.at[:, :, pl.ds(lane * 128, 128)], pair_refs[part].at[which, 0, :, slot], sem.at[0, lane]))
                copies.append(pltpu.make_async_copy(acc2.at[:, slot // wide, :, pl.ds(col * 128, 128)], pair_refs[part].at[which, 1, :, slot], sem.at[1, lane]))
            for copy in copies:
                copy.start()
            for copy in copies:
                copy.wait()

    hbm = pl.BlockSpec(memory_space=ANY)
    ops = [first, x, grad, act, slope, w_one, w_two]
    in_specs = [row_spec(d_model), row_spec(d_model), row_spec(d_ff), row_spec(d_ff), weight_spec(d_model, d_ff, which), weight_spec(d_ff, d_model, which)]
    alias = {}
    if pair is not None:
        alias = {len(ops) + part: 1 + part for part in range(n_part)}
        ops += pair
        in_specs += [hbm] * n_part
    out = pl.pallas_call(
        kernel,
        grid_spec=pltpu.PrefetchScalarGridSpec(
            num_scalar_prefetch=1, grid=(n_step,), in_specs=in_specs,
            out_specs=[row_spec(d_model)] + [hbm] * n_part,
            scratch_shapes=[pltpu.VMEM((major, 8, d_ff), F32), pltpu.VMEM((major, per, 8, d_model), F32), pltpu.SemaphoreType.DMA((2, lanes))]),
        out_shape=[jax.ShapeDtypeStruct((n_row, d_model), BF)] + [jax.ShapeDtypeStruct(pair_shape, F32)] * n_part,
        input_output_aliases=alias,
        compiler_params=pltpu.CompilerParams(vmem_limit_bytes=VMEM_CAP, dimension_semantics=("arbitrary",)),
        cost_estimate=pl.CostEstimate(flops=8 * n_row * d_model * d_ff, bytes_accessed=n_row * d_ff * 6, transcendentals=0),
        name="block_bwd",
    )(*ops)
    return out[0], list(out[1:])


def last_call(first, x, grad, act, slope, w_two, which, buf, part, n_part):
    n_row, d_model = grad.shape
    d_ff = w_two.shape[1]
    n_step = n_row // TM
    wide1, wide2 = d_ff // n_part, d_model // n_part
    major = d_model // 8
    per = d_ff // d_model

    def kernel(off_ref, x_ref, g_ref, a_ref, s_ref, w2_ref, old_ref, buf_ref, acc1, acc2, sem):
        step = pl.program_id(0)

        @pl.when(step == 0)
        def _():
            acc1[...] = jnp.zeros_like(acc1)
            acc2[...] = jnp.zeros_like(acc2)

        r = (dot_nt(g_ref[...], w2_ref[...]) * s_ref[...]).astype(BF)
        acc1[...] += dot_tn(x_ref[...], r).reshape(major, 8, wide1)
        acc2[...] += dot_tn(a_ref[...], g_ref[:, part * wide2:(part + 1) * wide2]).reshape(major, per, 8, wide2)

        @pl.when(step == n_step - 1)
        def _():
            copies = []
            for lane in range(wide1 // 128):
                tiles = wide2 // 128
                copies.append(pltpu.make_async_copy(acc1.at[:, :, pl.ds(lane * 128, 128)], buf_ref.at[which, 0, :, lane], sem.at[0, lane]))
                copies.append(pltpu.make_async_copy(acc2.at[:, lane // tiles, :, pl.ds(lane % tiles * 128, 128)], buf_ref.at[which, 1, :, lane], sem.at[1, lane]))
            for copy in copies:
                copy.start()
            for copy in copies:
                copy.wait()

    hbm = pl.BlockSpec(memory_space=ANY)
    part_spec = pl.BlockSpec((TM, wide1), lambda i, off: (i, part))
    w2_spec = pl.BlockSpec((None, wide1, d_model), lambda i, off: (which, part, 0), pipeline_mode=pl.Buffered(1))
    return pl.pallas_call(
        kernel,
        grid_spec=pltpu.PrefetchScalarGridSpec(
            num_scalar_prefetch=1, grid=(n_step,),
            in_specs=[row_spec(d_model, True), row_spec(d_model), row_spec(d_ff), part_spec, w2_spec, hbm],
            out_specs=hbm,
            scratch_shapes=[pltpu.VMEM((major, 8, wide1), F32), pltpu.VMEM((major, per, 8, wide2), F32), pltpu.SemaphoreType.DMA((2, wide1 // 128))]),
        out_shape=jax.ShapeDtypeStruct(buf.shape, F32),
        input_output_aliases={6: 0},
        compiler_params=pltpu.CompilerParams(vmem_limit_bytes=VMEM_CAP, dimension_semantics=("arbitrary",)),
        cost_estimate=pl.CostEstimate(flops=6 * n_row * d_model * wide1, bytes_accessed=n_row * d_ff * 4, transcendentals=0),
        name="block_last",
    )(first, x, grad, act, slope, w_two, buf)


def untile_rows(rows, r, c):
    return rows.reshape(r // 8, c // 128, 8, 128).transpose(0, 2, 1, 3).reshape(r, c)


def adam_call(grads, clip, w_old, m_old, v_old, strides, learn_rate):
    n_row = w_old.shape[0]
    blk = 2304
    n_half = n_row // blk // 2
    n_part = len(grads) - 1
    bc1 = 1.0 / (1.0 - BETA_ONE ** ADAM_STEP)
    bc2 = 1.0 / (1.0 - BETA_TWO ** ADAM_STEP)

    def kernel(c_ref, *refs):
        ga_refs, (gb_ref, w_ref, m_ref, v_ref, wn_ref, mn_ref, vn_ref, wb_ref) = refs[:n_part], refs[n_part:]
        clip_val = c_ref[0, 0]
        data_idx = lax.axis_index("data")

        def run(stride, g_refs):
            n = len(g_refs)
            share = stride // n
            def update(base, lo, tile):
                at = base // n + lo // n + tile % share * 8
                gc = clip_val * g_refs[tile // share][pl.ds(pl.multiple_of(at, 8), 8), :]
                flat = pl.ds(base + lo + tile, 8, stride=stride)
                w = w_ref[flat, :]
                m = BETA_ONE * m_ref[flat, :] + (1.0 - BETA_ONE) * gc
                v = BETA_TWO * v_ref[flat, :] + (1.0 - BETA_TWO) * gc * gc
                mn_ref[flat, :] = m
                vn_ref[flat, :] = v
                new = w - learn_rate * ((m * bc1) / (jnp.sqrt(v * bc2) + ADAM_EPS) + WEIGHT_DECAY * w)
                wn_ref[flat, :] = new
                return new

            def body(i, carry):
                base = pl.multiple_of(i * 192, 192)
                for lo in range(0, 192, 8 * stride):
                    for tile in range(0, stride, 2):
                        pair = jnp.concatenate([update(base, lo, tile), update(base, lo, tile + 1)], axis=0)
                        wb_ref[pl.ds(base + lo + tile * 8, 16), :] = pair.astype(BF)
                return carry

            lax.fori_loop(0, blk // 192, body, 0)

        for half, g_refs in enumerate((ga_refs, (gb_ref,))):
            for kind, stride in enumerate(strides):

                @pl.when((data_idx // 2 == kind) & (pl.program_id(0) // n_half == half))
                def _():
                    run(stride, g_refs)

    spec = pl.BlockSpec((blk, 128), lambda i: (i, 0))
    return pl.pallas_call(
        kernel, grid=(n_row // blk,),
        in_specs=[pl.BlockSpec(memory_space=pltpu.SMEM), *([pl.BlockSpec((blk // n_part, 128), lambda i: (jnp.minimum(i, n_half - 1), 0))] * n_part), pl.BlockSpec((blk, 128), lambda i: (jnp.maximum(i - n_half, 0), 0))] + [spec] * 3,
        out_specs=[spec] * 4,
        out_shape=[jax.ShapeDtypeStruct((n_row, 128), F32)] * 3 + [jax.ShapeDtypeStruct((n_row, 128), BF)],
        compiler_params=pltpu.CompilerParams(vmem_limit_bytes=VMEM_CAP, dimension_semantics=("arbitrary",)),
        name="adam",
    )(clip, *grads, w_old, m_old, v_old)


def solution(mesh):
    n_stage = mesh.shape["stage"]
    n_data = mesh.shape["data"]
    both = ("stage", "data")

    def device_step(x_loc, t_loc, w1_loc, w2_loc, wm_loc, m_loc, v_loc):
        n_micro, n_tok, d_model = x_loc.shape
        d_ff = w1_loc.shape[4]
        n_tokens = n_micro * n_tok * n_data
        n_blocks = 2 * n_stage
        tau_clip = 0.3 * d_model * math.sqrt(n_blocks * (3.0 / n_tokens + 0.008))
        learn_rate = 0.1 / math.sqrt(4.0 * d_model * n_blocks)
        stage_idx = lax.axis_index("stage")
        data_idx = lax.axis_index("data")
        n_mine = n_micro // n_stage
        n_row = n_mine * n_tok
        x_all = x_loc.reshape(n_micro * n_tok, d_model)
        t_all = t_loc.reshape(n_micro * n_tok, d_model)
        first = (stage_idx * (n_row // TM)).astype(jnp.int32).reshape(1)

        def gather(stack, half, after=None):
            part = stack.shape[3] // n_data
            mine = lax.dynamic_slice(stack, (0, half, 0, data_idx * part, 0), (1, 1, 1, part, stack.shape[4])).reshape(part, stack.shape[4])
            if after is not None:
                mine = lax.optimization_barrier((mine, after))[0]
            full = lax.all_gather(mine, both, axis=0, tiled=True)
            return full.reshape(n_stage, *stack.shape[3:])

        ones, twos = [None, None], [None, None]
        ones[0] = gather(w1_loc, 0)
        twos[0] = gather(w2_loc, 0, ones[0])
        ones[1] = gather(w1_loc, 1, twos[0])
        twos[1] = gather(w2_loc, 1, twos[0])

        cur, saved = x_all, []
        for blk in range(n_blocks):
            tail = dict(targets=t_all, n_tokens=n_tokens) if blk == n_blocks - 1 else {}
            if blk == 0:
                act, slope = up_call(first, cur, ones[0], 0, n_row)
                saved.append((cur, act, slope))
                cur = down_call(first, cur, act, twos[0], 0, n_row)
                continue
            outs = fwd_call(first, cur, ones[blk // 2], twos[blk // 2], blk % 2, n_row, **tail)
            saved.append((cur, outs[1], outs[2]))
            cur = outs[0]
        loss_acc = 0.5 * jnp.sum(outs[3])
        grad = cur

        def scatter(buf):
            return lax.psum_scatter(buf.reshape(n_stage * n_data, -1, 128), both, scatter_dimension=0, tiled=True)[0]

        def backward(blk, pair, n_part):
            inp, act, slope = saved[blk]
            return bwd_call(first, inp, grad, act, slope, ones[blk // 2], twos[blk // 2], blk % 2, pair, n_part)

        grad, pair = backward(3, None, 1)
        grad, pair = backward(2, pair, 1)
        late = scatter(pair[0])
        grad, bufs = backward(1, None, N_PART)
        inp, act, slope = saved[0]
        early = []
        for part in range(N_PART):
            early.append(scatter(last_call(first, inp, grad, act, slope, twos[0], 0, bufs[part], part, N_PART)))
        shards = early + [late]
        sq = sum(jnp.sum(s * s) for s in shards)
        sums = lax.psum(jnp.stack([sq, loss_acc]), both)
        clip = jnp.minimum(1.0, tau_clip / jnp.sqrt(sums[0])).reshape(1, 1)
        flat = lambda arr: arr.reshape(-1, 128)
        w_new, m_new, v_new, w_bf = adam_call(shards, clip, flat(wm_loc), flat(m_loc), flat(v_loc), (d_ff // 128, d_model // 128), learn_rate)
        w_full = lax.all_gather(w_bf.reshape(2, 1, -1, 128), "data", axis=1, tiled=True)
        w1_new = untile_rows(w_full[:, :2].reshape(-1, 128), 2 * d_model, d_ff).reshape(w1_loc.shape)
        w2_new = untile_rows(w_full[:, 2:].reshape(-1, 128), 2 * d_ff, d_model).reshape(w2_loc.shape)
        return w1_new, w2_new, w_new.reshape(wm_loc.shape), m_new.reshape(m_loc.shape), v_new.reshape(v_loc.shape), sums[1] / n_tokens

    act_spec = P(None, "data", None)
    flat_spec = P("stage", None, None, "data")
    return jax.shard_map(device_step, mesh=mesh, in_specs=(act_spec, act_spec, P("stage"), P("stage"), flat_spec, flat_spec, flat_spec), out_specs=(P("stage"), P("stage"), flat_spec, flat_spec, flat_spec, P()), check_vma=False)
```

time: 5550 us -> 1820 us (0.33)
  matrix products: 2940 us -> 0 us
  Pallas kernels: 0 us -> 1150 us
  waiting for transfers between devices: 1430 us -> 583 us
  other arithmetic: 666 us -> 11.5 us
  local copies, waits for them, and re-layouts: 270 us -> 21.5 us
  starting transfers between devices: 122 us -> 0.36 us
  loops' own time: 57.7 us -> 0 us
    dot_general x390 -> x0, matrix products: 2940 us -> none  [the longest x65 813 us: block_backward(): jnp.einsum('tf,td->fd', act_val.astype(jnp.bfloat16), grad_out, preferred...]
    pallas_call x0 -> x12, Pallas kernels: none -> 1150 us  [the longest x3 529 us: bwd_call(): pl.pallas_call(kernel, grid_spec=pltpu.PrefetchScalarGridSpec(num_scalar_...]
    unnamed x3 -> x9, waiting for transfers between devices: 622 us -> 1.32 us
    ppermute x130 -> x0, waiting for transfers between devices: 584 us -> none  [the longest x65 584 us: fwd_tick(): recv_act = lax.ppermute(h_cur, 'stage', fwd_perm)]
    reduce_scatter x0 -> x4, waiting for transfers between devices: none -> 358 us  [scatter(): lax.psum_scatter(buf.reshape(n_stage * n_data, -1, 128), both, scatter_di...]
    select_n x65 -> x0, other arithmetic: 182 us -> none  [bwd_tick(): grad_cur = jnp.where(active, grad_cur, jnp.zeros_like(grad_cur))]
    reduce_sum x66 -> x5, other arithmetic: 165 us -> 11.4 us  [the longest x4 10.8 us: device_step(): sq = sum((jnp.sum(s * s) for s in shards))]
    dynamic_update_slice x65 -> x0, other arithmetic: 144 us -> none  [fwd_tick(): lax.dynamic_update_slice(saved_in, h_cur[None, None, None], (half_idx, sl...]
  transfers between devices with their start and end apart: 132 -> 9, of which waited for: 68 -> 6; matrix products, arithmetic and copies ran while one was open for 29% -> 1% of each run, Pallas kernels for 0% -> 19%
where the time goes in v1:
time: 1820 us; the launch traced here: 1810 us
  Pallas kernels  1150 us (63%)
  waiting for transfers between devices  583 us (32%)
  blocking collectives  22.2 us (1%)
  local copies, waits for them, and re-layouts  21.5 us (1%)
  between operations  20.1 us (1%)
    pallas_call x3, Pallas kernels, bwd_call(): pl.pallas_call(kernel, grid_spec=pltpu.PrefetchScalarGridSpec(num_scalar_...  529 us
    reduce_scatter x4, waiting for transfers between devices, scatter(): lax.psum_scatter(buf.reshape(n_stage * n_data, -1, 128), both, scatter_di...  358 us
    pallas_call x3, Pallas kernels, fwd_call(): pl.pallas_call(kernel, grid_spec=pltpu.PrefetchScalarGridSpec(num_scalar_...  306 us
    pallas_call x3, Pallas kernels, last_call(): pl.pallas_call(kernel, grid_spec=pltpu.PrefetchScalarGridSpec(num_scalar_...  157 us
    all_gather x1, waiting for transfers between devices, device_step(): lax.all_gather(w_bf.reshape(2, 1, -1, 128), 'data', axis=1, tiled=True)  116 us
    all_gather x4, waiting for transfers between devices, gather(): full = lax.all_gather(mine, both, axis=0, tiled=True)  108 us
    pallas_call x1, Pallas kernels, up_call(): pl.pallas_call(kernel, grid_spec=pltpu.PrefetchScalarGridSpec(num_scalar_...  84 us
    pallas_call x1, Pallas kernels, down_call(): pl.pallas_call(kernel, grid_spec=pltpu.PrefetchScalarGridSpec(num_scalar_...  46.6 us
  transfers between devices with their start and end apart: 9, of which 6 were waited for; matrix products, arithmetic and copies ran while one was open for 1% of the time, Pallas kernels for 19%

profile of v1, /device:TPU:0, one launch (start us, length us, event | category | flops | bytes accessed | tf_op | source)
XLA Modules:
  0.0 1809.4 jit_solution(7958427001082167028)
XLA Ops:
  7.2 0.0 all-gather.15.cloned.1.call-start
  7.2 3.2 dynamic-slice_bitcast_fusion.1
  10.4 0.0 all-gather.15.cloned.1.call-update
  10.4 0.0 all-gather.7.cloned.1.call-start
  10.5 3.2 dynamic-slice_bitcast_fusion
  13.7 52.7 %all-gather.15.cloned.1.call-done = bf16[1,1,1,1536,3072]{4,3,2,1,0:T(8,128)(2,1)} async-done(((bf16[1,1,1,192,3072]{4,3,2,1,0:T(8,128)(2,1)}), bf16[1,1,1,1536,3072]{4,3,2,1,0:T(8,128)(2,1)}) %all-gather.15.cloned.1.call-update) | async-done | bytes 9437200 | tf_op jit(solution)/shard_map/all_gather | solution.py:357
  66.4 0.0 all-gather.7.cloned.1.call-update
  66.4 0.0 all-gather.9.cloned.1.call-start
  66.4 55.3 %all-gather.7.cloned.1.call-done = bf16[6144,768]{1,0:T(8,128)(2,1)} async-done(((bf16[768,768]{1,0:T(8,128)(2,1)}), bf16[6144,768]{1,0:T(8,128)(2,1)}) %all-gather.7.cloned.1.call-update) | async-done | bytes 9437200 | tf_op jit(solution)/shard_map/all_gather | solution.py:357
  121.7 0.0 all-gather.9.cloned.1.call-update
  121.7 0.0 all-gather.11.cloned.1.call-start
  121.8 0.5 all-gather.11.cloned.1.call-update
  122.3 0.0 reduce-scatter.5.cloned.1.call-start
  122.4 84.0 %block_up.1 = (bf16[8192,3072]{1,0:T(8,128)(2,1)}, f32[8192,3072]{1,0:T(8,128)}) custom-call(s32[1]{0:T(128)} %bitcast.off_ref, bf16[16384,768]{1,0:T(8,128)(2,1)} %bitcast.48, bf16[2,768,3072]{2,1,0:T(8,128)(2,1)} %bitcast.74), custom_call_target="tpu_custom_call" | custom-call | flops 38654705664 | bytes 150994944 | tf_op jit(solution)/shard_map/block_up/pallas_call | solution.py:120
  206.4 46.6 %block_down.1.x_ref = bf16[8192,768]{1,0:T(8,128)(2,1)} custom-call(s32[1]{0:T(128)} %bitcast.off_ref, bf16[16384,768]{1,0:T(8,128)(2,1)} %bitcast.49, bf16[8192,3072]{1,0:T(8,128)(2,1)} %get-tuple-element.33.a_ref, bf16[2,3072,768]{2,1,0:T(8,128)(2,1)} %bitcast.53), custom_call_target="tpu_custom_call" | custom-call | flops 38654705664 | bytes 50331648 | tf_op jit(solution)/shard_map/block_down/pallas_call | solution.py:140
  252.9 100.4 %block_fwd.3 = (bf16[8192,768]{1,0:T(8,128)(2,1)}, bf16[8192,3072]{1,0:T(8,128)(2,1)}, f32[8192,3072]{1,0:T(8,128)}) custom-call(s32[1]{0:T(128)} %bitcast.off_ref, bf16[8192,768]{1,0:T(8,128)(2,1)} %block_down.1.x_ref, bf16[2,768,3072]{2,1,0:T(8,128)(2,1)} %bitcast.75, bf16[2,3072,768]{2,1,0:T(8,128)(2,1)} %bitcast.54), custom_call_target="tpu_custom_call" | custom-call | flops 77309411328 | bytes 150994944 | tf_op jit(solution)/shard_map/block_fwd/pallas_call | solution.py:96
  353.3 0.0 all-gather.9.cloned.1.call-done
  353.3 0.0 all-gather.11.cloned.1.call-done
  353.3 101.2 %block_fwd.4 = (bf16[8192,768]{1,0:T(8,128)(2,1)}, bf16[8192,3072]{1,0:T(8,128)(2,1)}, f32[8192,3072]{1,0:T(8,128)}) custom-call(s32[1]{0:T(128)} %bitcast.off_ref, bf16[8192,768]{1,0:T(8,128)(2,1)} %get-tuple-element.35.x_ref, bf16[2,768,3072]{2,1,0:T(8,128)(2,1)} %bitcast.77, bf16[2,3072,768]{2,1,0:T(8,128)(2,1)} %bitcast.81), custom_call_target="tpu_custom_call" | custom-call | flops 77309411328 | bytes 150994944 | tf_op jit(solution)/shard_map/block_fwd/pallas_call | solution.py:96
  454.5 104.1 %block_fwd.5 = (bf16[8192,768]{1,0:T(8,128)(2,1)}, bf16[8192,3072]{1,0:T(8,128)(2,1)}, f32[8192,3072]{1,0:T(8,128)}, f32[8,768]{1,0:T(8,128)}) custom-call(s32[1]{0:T(128)} %bitcast.off_ref, bf16[8192,768]{1,0:T(8,128)(2,1)} %get-tuple-element.38.x_ref, bf16[2,768,3072]{2,1,0:T(8,128)(2,1)} %bitcast.78, bf16[2,3072,768]{2,1,0:T(8,128)(2,1)} %bitcast.82, ...), custom_call_target="tpu_custom_call" | custom-call | flops 77309411328 | bytes 150994944 | tf_op jit(solution)/shard_map/block_fwd/pallas_call | solution.py:96
  558.5 176.4 %block_bwd.3 = (bf16[8192,768]{1,0:T(8,128)(2,1)}, f32[2,2,96,24,8,128]{5,4,3,2,1,0:T(8,128)}) custom-call(s32[1]{0:T(128)} %bitcast.off_ref, bf16[8192,768]{1,0:T(8,128)(2,1)} %get-tuple-element.38.x_ref, bf16[8192,768]{1,0:T(8,128)(2,1)} %get-tuple-element.39.g_ref, bf16[8192,3072]{1,0:T(8,128)(2,1)} %get-tuple-element.40.a_ref, ...), custom_call_target="tpu_custom_call" | custom-call | flops 154618822656 | bytes 150994944 | tf_op jit(solution)/shard_map/block_bwd/pallas_call | solution.py:206
  735.0 176.4 %block_bwd.4 = (bf16[8192,768]{1,0:T(8,128)(2,1)}, f32[2,2,96,24,8,128]{5,4,3,2,1,0:T(8,128)}) custom-call(s32[1]{0:T(128)} %bitcast.off_ref, bf16[8192,768]{1,0:T(8,128)(2,1)} %get-tuple-element.35.x_ref, bf16[8192,768]{1,0:T(8,128)(2,1)} %get-tuple-element.42.g_ref, bf16[8192,3072]{1,0:T(8,128)(2,1)} %get-tuple-element.43.a_ref, ...), custom_call_target="tpu_custom_call", output_to_operand_aliasing={{1}: (7, {})} | custom-call | flops 154618822656 | bytes 150994944 | tf_op jit(solution)/shard_map/block_bwd/pallas_call | solution.py:206
  911.3 176.2 %block_bwd.5 = (bf16[8192,768]{1,0:T(8,128)(2,1)}, f32[2,2,96,8,8,128]{5,4,3,2,1,0:T(8,128)}, f32[2,2,96,8,8,128]{5,4,3,2,1,0:T(8,128)}, f32[2,2,96,8,8,128]{5,4,3,2,1,0:T(8,128)}) custom-call(s32[1]{0:T(128)} %bitcast.off_ref, bf16[8192,768]{1,0:T(8,128)(2,1)} %block_down.1.x_ref, bf16[8192,768]{1,0:T(8,128)(2,1)} %get-tuple-element.46.g_ref, ...), custom_call_target="tpu_custom_call" | custom-call | flops 154618822656 | bytes 150994944 | tf_op jit(solution)/shard_map/block_bwd/pallas_call | solution.py:206
  1087.5 52.5 %block_last.3 = f32[2,2,96,8,8,128]{5,4,3,2,1,0:T(8,128)} custom-call(s32[1]{0:T(128)} %bitcast.off_ref, bf16[16384,768]{1,0:T(8,128)(2,1)} %bitcast.50, bf16[8192,768]{1,0:T(8,128)(2,1)} %get-tuple-element.49.g_ref, bf16[8192,3072]{1,0:T(8,128)(2,1)} %get-tuple-element.33.a_ref, ...), custom_call_target="tpu_custom_call", output_to_operand_aliasing={{}: (6, {})} | custom-call | flops 38654705664 | bytes 100663296 | tf_op jit(solution)/shard_map/block_last/pallas_call | solution.py:256
  1140.0 0.0 reduce-scatter.5.cloned.1.call-update
  1140.0 0.0 reduce-scatter.7.cloned.1.call-start
  1140.1 52.3 %block_last.4 = f32[2,2,96,8,8,128]{5,4,3,2,1,0:T(8,128)} custom-call(s32[1]{0:T(128)} %bitcast.off_ref, bf16[16384,768]{1,0:T(8,128)(2,1)} %bitcast.51, bf16[8192,768]{1,0:T(8,128)(2,1)} %get-tuple-element.49.g_ref, bf16[8192,3072]{1,0:T(8,128)(2,1)} %get-tuple-element.33.a_ref, ...), custom_call_target="tpu_custom_call", output_to_operand_aliasing={{}: (6, {})} | custom-call | flops 38654705664 | bytes 100663296 | tf_op jit(solution)/shard_map/block_last/pallas_call | solution.py:256
  1192.4 0.0 reduce-scatter.7.cloned.1.call-update
  1192.4 0.0 reduce-scatter.9.cloned.1.call-start
  1192.4 52.2 %block_last.5 = f32[2,2,96,8,8,128]{5,4,3,2,1,0:T(8,128)} custom-call(s32[1]{0:T(128)} %bitcast.off_ref, bf16[16384,768]{1,0:T(8,128)(2,1)} %bitcast.52, bf16[8192,768]{1,0:T(8,128)(2,1)} %get-tuple-element.49.g_ref, bf16[8192,3072]{1,0:T(8,128)(2,1)} %get-tuple-element.33.a_ref, ...), custom_call_target="tpu_custom_call", output_to_operand_aliasing={{}: (6, {})} | custom-call | flops 38654705664 | bytes 100663296 | tf_op jit(solution)/shard_map/block_last/pallas_call | solution.py:256
  1244.7 0.0 reduce-scatter.9.cloned.1.call-update
  1244.7 0.0 reduce-scatter.11.cloned.1.call-start
  1244.7 0.0 copy-start
  1244.7 0.7 reduce-scatter.11.cloned.1.call-update
  1245.4 0.0 all-gather.13.cloned.1.call-start
  1245.5 0.0 copy-done
  1245.5 0.6 reduce_sum.49
  1246.8 0.0 reduce-scatter.5.cloned.1.call-done
  1246.8 2.4 multiply_reduce_fusion.3
  1249.2 59.3 %reduce-scatter.7.cloned.1.call-done = f32[1,3072,128]{2,1,0:T(8,128)} async-done(((f32[8,3072,128]{2,1,0:T(8,128)}), f32[1,3072,128]{2,1,0:T(8,128)}) %reduce-scatter.7.cloned.1.call-update) | async-done | bytes 1572880 | tf_op jit(solution)/shard_map/reduce_scatter | solution.py:381
  1308.5 2.4 multiply_reduce_fusion.2
  1312.2 82.2 %reduce-scatter.9.cloned.1.call-done = f32[1,3072,128]{2,1,0:T(8,128)} async-done(((f32[8,3072,128]{2,1,0:T(8,128)}), f32[1,3072,128]{2,1,0:T(8,128)}) %reduce-scatter.9.cloned.1.call-update) | async-done | bytes 1572880 | tf_op jit(solution)/shard_map/reduce_scatter | solution.py:381
  1394.5 2.4 multiply_reduce_fusion.1
  1397.5 216.8 %reduce-scatter.11.cloned.1.call-done = f32[1,9216,128]{2,1,0:T(8,128)} async-done(((f32[8,9216,128]{2,1,0:T(8,128)}), f32[1,9216,128]{2,1,0:T(8,128)}) %reduce-scatter.11.cloned.1.call-update) | async-done | bytes 4718608 | tf_op jit(solution)/shard_map/reduce_scatter | solution.py:381
  1614.3 3.6 multiply_reduce_fusion
  1618.6 0.1 pad_maximum_fusion
  1618.6 22.2 %psum.7 = f32[2]{0:T(128)S(1)} all-reduce(f32[2]{0:T(128)S(1)} %pad_maximum_fusion), channel_id=1, replica_groups=mesh['stage'=2,'data'=4] {'stage','data'}, use_global_device_ids=true, to_apply=%region_9.0 | all-reduce | flops 2 | bytes 16 | tf_op jit(solution)/shard_map/psum | solution.py:397
  1640.8 0.6 fusion.1
  1642.1 28.2 %adam.1 = (f32[18432,128]{1,0:T(8,128)}, f32[18432,128]{1,0:T(8,128)}, f32[18432,128]{1,0:T(8,128)}, bf16[18432,128]{1,0:T(8,128)(2,1)}) custom-call(f32[1,1]{1,0:T(1,128)} %bitcast.20.c_ref, f32[3072,128]{1,0:T(8,128)} %bitcast.69, f32[3072,128]{1,0:T(8,128)} %bitcast.70, f32[3072,128]{1,0:T(8,128)} %bitcast.71, f32[9216,128]{1,0:T(8,128)} %bitcast.63, ...), custom_call_target="tpu_custom_call" | custom-call | tf_op jit(solution)/shard_map/adam/pallas_call | solution.py:322
  1670.3 0.0 all-gather.13.cloned.1.call-update
  1670.9 115.8 %all-gather.13.cloned.1.call-done = bf16[2,4,9216,128]{3,2,1,0:T(8,128)(2,1)} async-done(((bf16[2,1,9216,128]{3,2,1,0:T(8,128)(2,1)}), bf16[2,4,9216,128]{3,2,1,0:T(8,128)(2,1)}) %all-gather.13.cloned.1.call-update) | async-done | bytes 18874384 | tf_op jit(solution)/shard_map/all_gather | solution.py:401
  1786.7 14.6 fusion
Async XLA Ops:
  7.2 59.2 %all-gather.15.cloned.1.call-start = ((), (), s32[]{:S(2)}) async-start(), calls=%async_computation.12 | async-start | bytes 10616832 | tf_op jit(solution)/shard_map/all_gather | solution.py:357
  10.4 111.3 %all-gather.7.cloned.1.call-start = ((), (), s32[]{:S(2)}) async-start(), calls=%async_computation.4 | async-start | bytes 10616832 | tf_op jit(solution)/shard_map/all_gather | solution.py:357
  66.4 286.9 %all-gather.9.cloned.1.call-start = ((), (), s32[]{:S(2)}) async-start(), calls=%async_computation.5 | async-start | bytes 10616832 | tf_op jit(solution)/shard_map/all_gather | solution.py:357
  121.7 231.6 %all-gather.11.cloned.1.call-start = ((), (), s32[]{:S(2)}) async-start(), calls=%async_computation.6 | async-start | bytes 10616832 | tf_op jit(solution)/shard_map/all_gather | solution.py:357
  122.3 1124.5 %reduce-scatter.5.cloned.1.call-start = ((), (), s32[]{:S(2)}) async-start(), calls=%async_computation.7 | async-start | bytes 14155776 | tf_op jit(solution)/shard_map/reduce_scatter | solution.py:381
  1140.0 168.5 %reduce-scatter.7.cloned.1.call-start = ((), (), s32[]{:S(2)}) async-start(), calls=%async_computation.8 | async-start | bytes 14155776 | tf_op jit(solution)/shard_map/reduce_scatter | solution.py:381
  1192.4 202.1 %reduce-scatter.9.cloned.1.call-start = ((), (), s32[]{:S(2)}) async-start(), calls=%async_computation.9 | async-start | bytes 14155776 | tf_op jit(solution)/shard_map/reduce_scatter | solution.py:381
  1244.7 369.6 %reduce-scatter.11.cloned.1.call-start = ((), (), s32[]{:S(2)}) async-start(), calls=%async_computation.10 | async-start | bytes 42467328 | tf_op jit(solution)/shard_map/reduce_scatter | solution.py:381
  1244.7 0.8 copy-start
  1245.4 541.3 %all-gather.13.cloned.1.call-start = ((), (), s32[]{:S(2)}) async-start(), calls=%async_computation.11 | async-start | bytes 23592960 | tf_op jit(solution)/shard_map/all_gather | solution.py:401
Sparse Core Ops, SparseCore 0:
  10.5 55.7 all-gather.14
  68.7 52.9 all-gather.6
  124.1 52.9 all-gather.8
  179.3 53.0 all-gather.10
  1140.2 82.4 reduce-scatter.4
  1226.0 82.4 reduce-scatter.6
  1311.9 82.4 reduce-scatter.8
  1398.0 216.2 reduce-scatter.10
  1670.4 116.2 all-gather.12

commit v2 on v1

--- a/solution.py
+++ b/solution.py
@@ -35,7 +35,7 @@
 
 def gelu_and_slope(u):
     sq = u * u
-    half = 0.5 + 0.5 * jnp.tanh(u * (K_GELU + (K_GELU * C_GELU) * sq))
+    half = jax.nn.sigmoid(u * (2.0 * K_GELU + (2.0 * K_GELU * C_GELU) * sq))
     act = u * half
     slope = half + (act * (1.0 - half)) * (2.0 * K_GELU + (6.0 * K_GELU * C_GELU) * sq)
     return act, slope
@@ -111,11 +111,14 @@
     d_ff = w_one.shape[2]
 
     def kernel(off_ref, x_ref, w1_ref, a_ref, s_ref):
+        pre = dot_nn(x_ref[...], w1_ref[:, :chunk])
         for lo in range(0, d_ff, chunk):
             cols = slice(lo, lo + chunk)
-            act, slope = gelu_and_slope(dot_nn(x_ref[...], w1_ref[:, cols]))
+            ahead = dot_nn(x_ref[...], w1_ref[:, lo + chunk:lo + 2 * chunk]) if lo + chunk < d_ff else None
+            act, slope = gelu_and_slope(pre)
             a_ref[:, cols] = act.astype(BF)
             s_ref[:, cols] = slope
+            pre = ahead
 
     return pl.pallas_call(
         kernel,
@@ -268,28 +271,24 @@
     )(first, x, grad, act, slope, w_two, buf)
 
 
-def untile_rows(rows, r, c):
-    return rows.reshape(r // 8, c // 128, 8, 128).transpose(0, 2, 1, 3).reshape(r, c)
-
-
-def adam_call(grads, clip, w_old, m_old, v_old, strides, learn_rate):
+def adam_call(grads, clip, w_old, m_old, v_old, half, filled, strides, learn_rate):
     n_row = w_old.shape[0]
     blk = 2304
     n_half = n_row // blk // 2
-    n_part = len(grads) - 1
+    n_part = len(grads)
     bc1 = 1.0 / (1.0 - BETA_ONE ** ADAM_STEP)
     bc2 = 1.0 / (1.0 - BETA_TWO ** ADAM_STEP)
 
     def kernel(c_ref, *refs):
-        ga_refs, (gb_ref, w_ref, m_ref, v_ref, wn_ref, mn_ref, vn_ref, wb_ref) = refs[:n_part], refs[n_part:]
+        g_refs, (w_ref, m_ref, v_ref), (wn_ref, mn_ref, vn_ref, wb_ref) = refs[:n_part], refs[n_part:n_part + 3], refs[-4:]
         clip_val = c_ref[0, 0]
         data_idx = lax.axis_index("data")
 
-        def run(stride, g_refs):
-            n = len(g_refs)
-            share = stride // n
+        def run(stride):
+            share = stride // n_part
+
             def update(base, lo, tile):
-                at = base // n + lo // n + tile % share * 8
+                at = base // n_part + lo // n_part + tile % share * 8
                 gc = clip_val * g_refs[tile // share][pl.ds(pl.multiple_of(at, 8), 8), :]
                 flat = pl.ds(base + lo + tile, 8, stride=stride)
                 w = w_ref[flat, :]
@@ -311,22 +310,88 @@
 
             lax.fori_loop(0, blk // 192, body, 0)
 
-        for half, g_refs in enumerate((ga_refs, (gb_ref,))):
-            for kind, stride in enumerate(strides):
-
-                @pl.when((data_idx // 2 == kind) & (pl.program_id(0) // n_half == half))
-                def _():
-                    run(stride, g_refs)
-
-    spec = pl.BlockSpec((blk, 128), lambda i: (i, 0))
-    return pl.pallas_call(
-        kernel, grid=(n_row // blk,),
-        in_specs=[pl.BlockSpec(memory_space=pltpu.SMEM), *([pl.BlockSpec((blk // n_part, 128), lambda i: (jnp.minimum(i, n_half - 1), 0))] * n_part), pl.BlockSpec((blk, 128), lambda i: (jnp.maximum(i - n_half, 0), 0))] + [spec] * 3,
-        out_specs=[spec] * 4,
-        out_shape=[jax.ShapeDtypeStruct((n_row, 128), F32)] * 3 + [jax.ShapeDtypeStruct((n_row, 128), BF)],
-        compiler_params=pltpu.CompilerParams(vmem_limit_bytes=VMEM_CAP, dimension_semantics=("arbitrary",)),
+        for kind, stride in enumerate(strides):
+
+            @pl.when(data_idx // 2 == kind)
+            def _():
+                run(stride)
+
+    spec = pl.BlockSpec((blk, 128), lambda i: (i + half * n_half, 0))
+    hbm = pl.BlockSpec(memory_space=ANY)
+    return pl.pallas_call(
+        kernel, grid=(n_half,),
+        in_specs=[pl.BlockSpec(memory_space=pltpu.SMEM)] + [pl.BlockSpec((blk // n_part, 128), lambda i: (i, 0))] * n_part + [spec] * 3 + [hbm] * len(filled),
+        out_specs=[spec] * 3 + [pl.BlockSpec((blk, 128), lambda i: (i, 0))],
+        out_shape=[jax.ShapeDtypeStruct((n_row, 128), F32)] * 3 + [jax.ShapeDtypeStruct((n_row // 2, 128), BF)],
+        input_output_aliases={4 + n_part + k: k for k in range(len(filled))},
+        compiler_params=pltpu.CompilerParams(vmem_limit_bytes=VMEM_CAP, dimension_semantics=("arbitrary",)),
+        cost_estimate=pl.CostEstimate(flops=20 * n_row * 64, bytes_accessed=n_row * 64 * 30, transcendentals=0),
         name="adam",
-    )(clip, *grads, w_old, m_old, v_old)
+    )(clip, *grads, w_old, m_old, v_old, *filled)
+
+
+def place_call(rows, half, filled, d_model, d_ff):
+    n_one = d_model * d_ff // 1024
+    lanes1, lanes2 = d_ff // 128, d_model // 128
+    steps = 12
+    step1, step2 = d_model // 8 // steps, d_ff // 8 // steps
+
+    def kernel(one_ref, two_ref, *refs):
+        w1_ref, w2_ref = refs[-2:]
+        for lane in range(lanes1):
+            w1_ref[:, :, lane * 128:(lane + 1) * 128] = one_ref[:, lane]
+        for lane in range(lanes2):
+            w2_ref[:, :, lane * 128:(lane + 1) * 128] = two_ref[:, lane]
+
+    hbm = pl.BlockSpec(memory_space=ANY)
+    return pl.pallas_call(
+        kernel, grid=(steps,),
+        in_specs=[pl.BlockSpec((step1, lanes1, 8, 128), lambda i: (i, 0, 0, 0)), pl.BlockSpec((step2, lanes2, 8, 128), lambda i: (steps + i, 0, 0, 0))] + [hbm] * len(filled),
+        out_specs=[pl.BlockSpec((None, step1, 8, d_ff), lambda i: (half, i, 0, 0)), pl.BlockSpec((None, step2, 8, d_model), lambda i: (half, i, 0, 0))],
+        out_shape=[jax.ShapeDtypeStruct((2, d_model // 8, 8, d_ff), BF), jax.ShapeDtypeStruct((2, d_ff // 8, 8, d_model), BF)],
+        input_output_aliases={2 + k: k for k in range(len(filled))},
+        compiler_params=pltpu.CompilerParams(vmem_limit_bytes=VMEM_CAP, dimension_semantics=("arbitrary",)),
+        cost_estimate=pl.CostEstimate(flops=n_one * 1024, bytes_accessed=n_one * 8192, transcendentals=0),
+        name="place",
+    )(rows.reshape(-1, lanes1, 8, 128), rows.reshape(-1, lanes2, 8, 128), *filled)
+
+
+def sum_call(part, n_stage, n_data):
+    n_dev = n_stage * n_data
+
+    def kernel(x_ref, o_ref, slots, send_sem, recv_sem):
+        me = lax.axis_index("stage") * n_data + lax.axis_index("data")
+        barrier = pltpu.get_barrier_semaphore()
+        peers = []
+        for k in range(1, n_dev):
+            other = lax.rem(me + k, n_dev)
+            peers.append((lax.div(other, n_data), lax.rem(other, n_data)))
+        for peer in peers:
+            pl.semaphore_signal(barrier, inc=1, device_id=peer, device_id_type=pl.DeviceIdType.MESH)
+        pl.semaphore_wait(barrier, n_dev - 1)
+        copies = []
+        for k, peer in enumerate(peers, 1):
+            copies.append(pltpu.make_async_remote_copy(
+                src_ref=x_ref, dst_ref=slots.at[k], send_sem=send_sem.at[k], recv_sem=recv_sem.at[k],
+                device_id=peer, device_id_type=pl.DeviceIdType.MESH))
+        for copy in copies:
+            copy.start()
+        slots[0] = x_ref[...]
+        for copy in copies:
+            copy.wait()
+        total = jnp.zeros_like(x_ref)
+        for dev in range(n_dev):
+            total = total + slots[lax.rem(me - dev + n_dev, n_dev)]
+        o_ref[...] = total
+
+    vmem = pl.BlockSpec(memory_space=pltpu.VMEM)
+    return pl.pallas_call(
+        kernel, in_specs=[vmem], out_specs=vmem,
+        out_shape=jax.ShapeDtypeStruct(part.shape, F32),
+        scratch_shapes=[pltpu.VMEM((n_dev, *part.shape), F32), pltpu.SemaphoreType.DMA((n_dev,)), pltpu.SemaphoreType.DMA((n_dev,))],
+        compiler_params=pltpu.CompilerParams(collective_id=0, has_side_effects=True),
+        name="small_sum",
+    )(part)
 
 
 def solution(mesh):
@@ -374,7 +439,7 @@
             outs = fwd_call(first, cur, ones[blk // 2], twos[blk // 2], blk % 2, n_row, **tail)
             saved.append((cur, outs[1], outs[2]))
             cur = outs[0]
-        loss_acc = 0.5 * jnp.sum(outs[3])
+        loss_rows = jnp.sum(outs[3].reshape(8, -1, 128), axis=1)
         grad = cur
 
         def scatter(buf):
@@ -391,17 +456,27 @@
         inp, act, slope = saved[0]
         early = []
         for part in range(N_PART):
-            early.append(scatter(last_call(first, inp, grad, act, slope, twos[0], 0, bufs[part], part, N_PART)))
-        shards = early + [late]
-        sq = sum(jnp.sum(s * s) for s in shards)
-        sums = lax.psum(jnp.stack([sq, loss_acc]), both)
-        clip = jnp.minimum(1.0, tau_clip / jnp.sqrt(sums[0])).reshape(1, 1)
+            buf = last_call(first, inp, grad, act, slope, twos[0], 0, bufs[part], part, N_PART)
+            early.append(scatter(buf))
+        fold = lambda arr: jnp.sum(arr.reshape(-1, 8, 128), axis=0)
+        squares = sum(fold(shard * shard) for shard in [late] + early)
+        sums = sum_call(jnp.concatenate([squares, loss_rows], 0), n_stage, n_data)
+        clip = jnp.minimum(1.0, tau_clip / jnp.sqrt(jnp.sum(sums[:8]))).reshape(1, 1)
+        mean_loss = 0.5 * jnp.sum(sums[8:]) / n_tokens
         flat = lambda arr: arr.reshape(-1, 128)
-        w_new, m_new, v_new, w_bf = adam_call(shards, clip, flat(wm_loc), flat(m_loc), flat(v_loc), (d_ff // 128, d_model // 128), learn_rate)
-        w_full = lax.all_gather(w_bf.reshape(2, 1, -1, 128), "data", axis=1, tiled=True)
-        w1_new = untile_rows(w_full[:, :2].reshape(-1, 128), 2 * d_model, d_ff).reshape(w1_loc.shape)
-        w2_new = untile_rows(w_full[:, 2:].reshape(-1, 128), 2 * d_ff, d_model).reshape(w2_loc.shape)
-        return w1_new, w2_new, w_new.reshape(wm_loc.shape), m_new.reshape(m_loc.shape), v_new.reshape(v_loc.shape), sums[1] / n_tokens
+        strides = (d_ff // 128, d_model // 128)
+        state = [flat(wm_loc), flat(m_loc), flat(v_loc)]
+        filled, full = [], [None, None]
+        for half, grads in ((1, [late]), (0, early)):
+            *filled, w_bf = adam_call(grads, clip, *state, half, filled, strides, learn_rate)
+            full[half] = lax.all_gather(w_bf, "data", axis=0, tiled=True)
+        w_new, m_new, v_new = filled
+        placed = []
+        for half in (1, 0):
+            placed = place_call(full[half], half, placed, d_model, d_ff)
+        w1_new = placed[0].reshape(w1_loc.shape)
+        w2_new = placed[1].reshape(w2_loc.shape)
+        return w1_new, w2_new, w_new.reshape(wm_loc.shape), m_new.reshape(m_loc.shape), v_new.reshape(v_loc.shape), mean_loss
 
     act_spec = P(None, "data", None)
     flat_spec = P("stage", None, None, "data")

time: 1820 us -> 1790 us (0.984)
  Pallas kernels: 1150 us -> 1180 us
  blocking collectives: 22.2 us -> 0 us
    pallas_call x1 -> x5, Pallas kernels: 28.2 us -> 59.4 us  [the longest x2 30.1 us: adam_call(): pl.pallas_call(kernel, grid=(n_half,), in_specs=[pl.BlockSpec(memory_spac...]
    psum x1 -> x0, blocking collectives: 22.2 us -> none  [device_step(): sums = lax.psum(jnp.stack([sq, loss_acc]), both)]
    all_gather x1 -> x2, waiting for transfers between devices: 116 us -> 96.1 us  [device_step(): full[half] = lax.all_gather(w_bf, 'data', axis=0, tiled=True)]
  transfers between devices with their start and end apart: 9 -> 10, of which waited for: 6 -> 7; matrix products, arithmetic and copies ran while one was open for 1% -> 0% of each run, Pallas kernels for 19% -> 21%
where the time goes in v2:
time: 1790 us; the launch traced here: 1780 us
  Pallas kernels  1180 us (66%)
  waiting for transfers between devices  566 us (32%)
    pallas_call x3, Pallas kernels, bwd_call(): pl.pallas_call(kernel, grid_spec=pltpu.PrefetchScalarGridSpec(num_scalar_...  529 us
    reduce_scatter x4, waiting for transfers between devices, scatter(): lax.psum_scatter(buf.reshape(n_stage * n_data, -1, 128), both, scatter_di...  361 us
    pallas_call x3, Pallas kernels, fwd_call(): pl.pallas_call(kernel, grid_spec=pltpu.PrefetchScalarGridSpec(num_scalar_...  293 us
    pallas_call x3, Pallas kernels, last_call(): pl.pallas_call(kernel, grid_spec=pltpu.PrefetchScalarGridSpec(num_scalar_...  166 us
    all_gather x4, waiting for transfers between devices, gather(): full = lax.all_gather(mine, both, axis=0, tiled=True)  108 us
    all_gather x2, waiting for transfers between devices, device_step(): full[half] = lax.all_gather(w_bf, 'data', axis=0, tiled=True)  96.1 us
    pallas_call x1, Pallas kernels, up_call(): pl.pallas_call(kernel, grid_spec=pltpu.PrefetchScalarGridSpec(num_scalar_...  80.6 us
    pallas_call x1, Pallas kernels, down_call(): pl.pallas_call(kernel, grid_spec=pltpu.PrefetchScalarGridSpec(num_scalar_...  47.5 us
  transfers between devices with their start and end apart: 10, of which 7 were waited for; matrix products, arithmetic and copies ran while one was open for 0% of the time, Pallas kernels for 21%

profile of v2, /device:TPU:0, one launch (start us, length us, event | category | flops | bytes accessed | tf_op | source)
XLA Modules:
  0.0 1775.9 jit_solution(4389299369163565198)
XLA Ops:
  7.2 0.0 all-gather.18.cloned.1.call-start
  7.2 3.2 dynamic-slice_bitcast_fusion.1
  10.4 0.0 all-gather.18.cloned.1.call-update
  10.4 0.0 all-gather.8.cloned.1.call-start
  10.5 3.2 dynamic-slice_bitcast_fusion
  13.7 52.8 %all-gather.18.cloned.1.call-done = bf16[1,1,1,1536,3072]{4,3,2,1,0:T(8,128)(2,1)} async-done(((bf16[1,1,1,192,3072]{4,3,2,1,0:T(8,128)(2,1)}), bf16[1,1,1,1536,3072]{4,3,2,1,0:T(8,128)(2,1)}) %all-gather.18.cloned.1.call-update) | async-done | bytes 9437200 | tf_op jit(solution)/shard_map/all_gather | solution.py:422
  66.5 0.0 all-gather.8.cloned.1.call-update
  66.5 0.0 all-gather.10.cloned.1.call-start
  66.6 55.5 %all-gather.8.cloned.1.call-done = bf16[6144,768]{1,0:T(8,128)(2,1)} async-done(((bf16[768,768]{1,0:T(8,128)(2,1)}), bf16[6144,768]{1,0:T(8,128)(2,1)}) %all-gather.8.cloned.1.call-update) | async-done | bytes 9437200 | tf_op jit(solution)/shard_map/all_gather | solution.py:422
  122.1 0.0 all-gather.10.cloned.1.call-update
  122.1 0.0 all-gather.12.cloned.1.call-start
  122.1 0.5 all-gather.12.cloned.1.call-update
  122.7 0.0 reduce-scatter.11.cloned.1.call-start
  122.7 80.6 %block_up.1 = (bf16[8192,3072]{1,0:T(8,128)(2,1)}, f32[8192,3072]{1,0:T(8,128)}) custom-call(s32[1]{0:T(128)} %bitcast.off_ref, bf16[16384,768]{1,0:T(8,128)(2,1)} %bitcast.48, bf16[2,768,3072]{2,1,0:T(8,128)(2,1)} %bitcast.83), custom_call_target="tpu_custom_call" | custom-call | flops 38654705664 | bytes 150994944 | tf_op jit(solution)/shard_map/block_up/pallas_call | solution.py:123
  203.3 47.5 %block_down.1.x_ref = bf16[8192,768]{1,0:T(8,128)(2,1)} custom-call(s32[1]{0:T(128)} %bitcast.off_ref, bf16[16384,768]{1,0:T(8,128)(2,1)} %bitcast.49, bf16[8192,3072]{1,0:T(8,128)(2,1)} %get-tuple-element.41.a_ref, bf16[2,3072,768]{2,1,0:T(8,128)(2,1)} %bitcast.53), custom_call_target="tpu_custom_call" | custom-call | flops 38654705664 | bytes 50331648 | tf_op jit(solution)/shard_map/block_down/pallas_call | solution.py:143
  250.8 96.2 %block_fwd.3 = (bf16[8192,768]{1,0:T(8,128)(2,1)}, bf16[8192,3072]{1,0:T(8,128)(2,1)}, f32[8192,3072]{1,0:T(8,128)}) custom-call(s32[1]{0:T(128)} %bitcast.off_ref, bf16[8192,768]{1,0:T(8,128)(2,1)} %block_down.1.x_ref, bf16[2,768,3072]{2,1,0:T(8,128)(2,1)} %bitcast.84, bf16[2,3072,768]{2,1,0:T(8,128)(2,1)} %bitcast.54), custom_call_target="tpu_custom_call" | custom-call | flops 77309411328 | bytes 150994944 | tf_op jit(solution)/shard_map/block_fwd/pallas_call | solution.py:96
  347.1 0.0 all-gather.10.cloned.1.call-done
  347.1 0.0 all-gather.12.cloned.1.call-done
  347.1 96.5 %block_fwd.4 = (bf16[8192,768]{1,0:T(8,128)(2,1)}, bf16[8192,3072]{1,0:T(8,128)(2,1)}, f32[8192,3072]{1,0:T(8,128)}) custom-call(s32[1]{0:T(128)} %bitcast.off_ref, bf16[8192,768]{1,0:T(8,128)(2,1)} %get-tuple-element.43.x_ref, bf16[2,768,3072]{2,1,0:T(8,128)(2,1)} %bitcast.86, bf16[2,3072,768]{2,1,0:T(8,128)(2,1)} %bitcast.90), custom_call_target="tpu_custom_call" | custom-call | flops 77309411328 | bytes 150994944 | tf_op jit(solution)/shard_map/block_fwd/pallas_call | solution.py:96
  443.6 100.1 %block_fwd.5 = (bf16[8192,768]{1,0:T(8,128)(2,1)}, bf16[8192,3072]{1,0:T(8,128)(2,1)}, f32[8192,3072]{1,0:T(8,128)}, f32[8,768]{1,0:T(8,128)}) custom-call(s32[1]{0:T(128)} %bitcast.off_ref, bf16[8192,768]{1,0:T(8,128)(2,1)} %get-tuple-element.46.x_ref, bf16[2,768,3072]{2,1,0:T(8,128)(2,1)} %bitcast.87, bf16[2,3072,768]{2,1,0:T(8,128)(2,1)} %bitcast.91, ...), custom_call_target="tpu_custom_call" | custom-call | flops 77309411328 | bytes 150994944 | tf_op jit(solution)/shard_map/block_fwd/pallas_call | solution.py:96
  543.7 176.4 %block_bwd.3 = (bf16[8192,768]{1,0:T(8,128)(2,1)}, f32[2,2,96,24,8,128]{5,4,3,2,1,0:T(8,128)}) custom-call(s32[1]{0:T(128)} %bitcast.off_ref, bf16[8192,768]{1,0:T(8,128)(2,1)} %get-tuple-element.46.x_ref, bf16[8192,768]{1,0:T(8,128)(2,1)} %get-tuple-element.47.g_ref, bf16[8192,3072]{1,0:T(8,128)(2,1)} %get-tuple-element.48.a_ref, ...), custom_call_target="tpu_custom_call" | custom-call | flops 154618822656 | bytes 150994944 | tf_op jit(solution)/shard_map/block_bwd/pallas_call | solution.py:209
  720.1 176.5 %block_bwd.4 = (bf16[8192,768]{1,0:T(8,128)(2,1)}, f32[2,2,96,24,8,128]{5,4,3,2,1,0:T(8,128)}) custom-call(s32[1]{0:T(128)} %bitcast.off_ref, bf16[8192,768]{1,0:T(8,128)(2,1)} %get-tuple-element.43.x_ref, bf16[8192,768]{1,0:T(8,128)(2,1)} %get-tuple-element.50.g_ref, bf16[8192,3072]{1,0:T(8,128)(2,1)} %get-tuple-element.51.a_ref, ...), custom_call_target="tpu_custom_call", output_to_operand_aliasing={{1}: (7, {})} | custom-call | flops 154618822656 | bytes 150994944 | tf_op jit(solution)/shard_map/block_bwd/pallas_call | solution.py:209
  896.6 176.3 %block_bwd.5 = (bf16[8192,768]{1,0:T(8,128)(2,1)}, f32[2,2,96,8,8,128]{5,4,3,2,1,0:T(8,128)}, f32[2,2,96,8,8,128]{5,4,3,2,1,0:T(8,128)}, f32[2,2,96,8,8,128]{5,4,3,2,1,0:T(8,128)}) custom-call(s32[1]{0:T(128)} %bitcast.off_ref, bf16[8192,768]{1,0:T(8,128)(2,1)} %block_down.1.x_ref, bf16[8192,768]{1,0:T(8,128)(2,1)} %get-tuple-element.55.g_ref, ...), custom_call_target="tpu_custom_call" | custom-call | flops 154618822656 | bytes 150994944 | tf_op jit(solution)/shard_map/block_bwd/pallas_call | solution.py:209
  1072.9 52.5 %block_last.5 = f32[2,2,96,8,8,128]{5,4,3,2,1,0:T(8,128)} custom-call(s32[1]{0:T(128)} %bitcast.off_ref, bf16[16384,768]{1,0:T(8,128)(2,1)} %bitcast.50, bf16[8192,768]{1,0:T(8,128)(2,1)} %get-tuple-element.58.g_ref, bf16[8192,3072]{1,0:T(8,128)(2,1)} %get-tuple-element.41.a_ref, ...), custom_call_target="tpu_custom_call", output_to_operand_aliasing={{}: (6, {})} | custom-call | flops 38654705664 | bytes 100663296 | tf_op jit(solution)/shard_map/block_last/pallas_call | solution.py:259
  1125.4 0.0 reduce-scatter.11.cloned.1.call-update
  1125.4 0.0 reduce-scatter.9.cloned.1.call-start
  1125.4 57.4 %block_last.4 = f32[2,2,96,8,8,128]{5,4,3,2,1,0:T(8,128)} custom-call(s32[1]{0:T(128)} %bitcast.off_ref, bf16[16384,768]{1,0:T(8,128)(2,1)} %bitcast.51, bf16[8192,768]{1,0:T(8,128)(2,1)} %get-tuple-element.58.g_ref, bf16[8192,3072]{1,0:T(8,128)(2,1)} %get-tuple-element.41.a_ref, ...), custom_call_target="tpu_custom_call", output_to_operand_aliasing={{}: (6, {})} | custom-call | flops 38654705664 | bytes 100663296 | tf_op jit(solution)/shard_map/block_last/pallas_call | solution.py:259
  1182.8 0.0 reduce-scatter.9.cloned.1.call-update
  1182.8 0.0 reduce-scatter.7.cloned.1.call-start
  1182.9 55.9 %block_last.3 = f32[2,2,96,8,8,128]{5,4,3,2,1,0:T(8,128)} custom-call(s32[1]{0:T(128)} %bitcast.off_ref, bf16[16384,768]{1,0:T(8,128)(2,1)} %bitcast.52, bf16[8192,768]{1,0:T(8,128)(2,1)} %get-tuple-element.58.g_ref, bf16[8192,3072]{1,0:T(8,128)(2,1)} %get-tuple-element.41.a_ref, ...), custom_call_target="tpu_custom_call", output_to_operand_aliasing={{}: (6, {})} | custom-call | flops 38654705664 | bytes 100663296 | tf_op jit(solution)/shard_map/block_last/pallas_call | solution.py:259
  1238.8 0.0 reduce-scatter.7.cloned.1.call-update
  1238.8 0.0 reduce-scatter.5.cloned.1.call-start
  1238.8 0.0 copy-start
  1238.8 0.7 reduce-scatter.5.cloned.1.call-update
  1239.5 0.0 all-gather.16.cloned.1.call-start
  1239.6 0.0 copy-done
  1239.6 0.0 reduce-scatter.11.cloned.1.call-done
  1239.6 1.8 bitcast_reduce_fusion.1
  1241.5 55.8 %reduce-scatter.9.cloned.1.call-done = f32[1,3072,128]{2,1,0:T(8,128)} async-done(((f32[8,3072,128]{2,1,0:T(8,128)}), f32[1,3072,128]{2,1,0:T(8,128)}) %reduce-scatter.9.cloned.1.call-update) | async-done | bytes 1572880 | tf_op jit(solution)/shard_map/reduce_scatter | solution.py:446
  1297.3 1.8 bitcast_reduce_fusion.2
  1299.1 85.6 %reduce-scatter.7.cloned.1.call-done = f32[1,3072,128]{2,1,0:T(8,128)} async-done(((f32[8,3072,128]{2,1,0:T(8,128)}), f32[1,3072,128]{2,1,0:T(8,128)}) %reduce-scatter.7.cloned.1.call-update) | async-done | bytes 1572880 | tf_op jit(solution)/shard_map/reduce_scatter | solution.py:446
  1384.7 1.8 bitcast_reduce_fusion.3
  1386.5 219.1 %reduce-scatter.5.cloned.1.call-done = f32[1,9216,128]{2,1,0:T(8,128)} async-done(((f32[8,9216,128]{2,1,0:T(8,128)}), f32[1,9216,128]{2,1,0:T(8,128)}) %reduce-scatter.5.cloned.1.call-update) | async-done | bytes 4718608 | tf_op jit(solution)/shard_map/reduce_scatter | solution.py:446
  1605.6 3.0 bitcast_reduce_fusion
  1608.6 0.6 pad_maximum_fusion.x_ref
  1609.2 6.2 small_sum.1
  1615.4 1.3 slice_reduce_fusion
  1617.4 14.5 adam.2
  1631.9 0.0 all-gather.16.cloned.1.call-update
  1631.9 0.0 all-gather.14.cloned.1.call-start
  1632.0 15.7 adam.3
  1647.6 0.0 all-gather.14.cloned.1.call-update
  1648.3 45.0 %all-gather.16.cloned.1.call-done = bf16[36864,128]{1,0:T(8,128)(2,1)} async-done(((bf16[9216,128]{1,0:T(8,128)(2,1)}), bf16[36864,128]{1,0:T(8,128)(2,1)}) %all-gather.16.cloned.1.call-update) | async-done | bytes 9437200 | tf_op jit(solution)/shard_map/all_gather | solution.py:472
  1693.3 11.7 place.2
  1705.0 51.1 %all-gather.14.cloned.1.call-done = bf16[36864,128]{1,0:T(8,128)(2,1)} async-done(((bf16[9216,128]{1,0:T(8,128)(2,1)}), bf16[36864,128]{1,0:T(8,128)(2,1)}) %all-gather.14.cloned.1.call-update) | async-done | bytes 9437200 | tf_op jit(solution)/shard_map/all_gather | solution.py:472
  1756.2 11.3 place.3
  (2 shorter events, 0.0 us)
Async XLA Ops:
  7.2 59.3 %all-gather.18.cloned.1.call-start = ((), (), s32[]{:S(2)}) async-start(), calls=%async_computation.13 | async-start | bytes 10616832 | tf_op jit(solution)/shard_map/all_gather | solution.py:422
  10.4 111.6 %all-gather.8.cloned.1.call-start = ((), (), s32[]{:S(2)}) async-start(), calls=%async_computation.4 | async-start | bytes 10616832 | tf_op jit(solution)/shard_map/all_gather | solution.py:422
  66.5 280.5 %all-gather.10.cloned.1.call-start = ((), (), s32[]{:S(2)}) async-start(), calls=%async_computation.5 | async-start | bytes 10616832 | tf_op jit(solution)/shard_map/all_gather | solution.py:422
  122.1 225.0 %all-gather.12.cloned.1.call-start = ((), (), s32[]{:S(2)}) async-start(), calls=%async_computation.6 | async-start | bytes 10616832 | tf_op jit(solution)/shard_map/all_gather | solution.py:422
  122.7 1117.0 %reduce-scatter.11.cloned.1.call-start = ((), (), s32[]{:S(2)}) async-start(), calls=%async_computation.10 | async-start | bytes 14155776 | tf_op jit(solution)/shard_map/reduce_scatter | solution.py:446
  1125.4 171.9 %reduce-scatter.9.cloned.1.call-start = ((), (), s32[]{:S(2)}) async-start(), calls=%async_computation.9 | async-start | bytes 14155776 | tf_op jit(solution)/shard_map/reduce_scatter | solution.py:446
  1182.8 201.9 %reduce-scatter.7.cloned.1.call-start = ((), (), s32[]{:S(2)}) async-start(), calls=%async_computation.8 | async-start | bytes 14155776 | tf_op jit(solution)/shard_map/reduce_scatter | solution.py:446
  1238.8 366.9 %reduce-scatter.5.cloned.1.call-start = ((), (), s32[]{:S(2)}) async-start(), calls=%async_computation.7 | async-start | bytes 42467328 | tf_op jit(solution)/shard_map/reduce_scatter | solution.py:446
  1238.8 0.8 copy-start
  1239.5 453.8 %all-gather.16.cloned.1.call-start = ((), (), s32[]{:S(2)}) async-start(), calls=%async_computation.12 | async-start | bytes 11796480 | tf_op jit(solution)/shard_map/all_gather | solution.py:472
  1631.9 124.3 %all-gather.14.cloned.1.call-start = ((), (), s32[]{:S(2)}) async-start(), calls=%async_computation.11 | async-start | bytes 11796480 | tf_op jit(solution)/shard_map/all_gather | solution.py:472
Sparse Core Ops, SparseCore 0:
  10.5 55.9 all-gather.17
  68.9 53.1 all-gather.7
  124.4 53.1 all-gather.9
  179.9 53.1 all-gather.11
  1125.5 84.4 reduce-scatter.10
  1213.3 83.9 reduce-scatter.8
  1300.7 83.9 reduce-scatter.6
  1388.3 217.3 reduce-scatter.4
  1632.0 61.2 all-gather.15
  1694.7 61.4 all-gather.13
